TPU v7x, 32 devices: a whole 2x2x4 slice. The times are simulated.
32 devices in a mesh: pod: 2 (over x), data: 4 (over z), expert: 4 (over y, core).
Axes of the slice: x: 2, y: 2, z: 4, core: 2. Of those that a mesh axis runs over, the one named last changes fastest.
Arguments:
- tokens: bfloat16 [16384, 1024], P(('pod', 'data', 'expert')), parts along dimension 0
- routes: int32 [16384, 8], P(('pod', 'data', 'expert')), parts along dimension 0
- gates: float32 [16384, 8], P(('pod', 'data', 'expert')), parts along dimension 0
- grad_y: bfloat16 [16384, 1024], P(('pod', 'data', 'expert')), parts along dimension 0
- w_in1: bfloat16 [32, 1024, 512], P('expert')
- w_in3: bfloat16 [32, 1024, 512], P('expert')
- w_out: bfloat16 [32, 512, 1024], P('expert')
Outputs:
- output 1: bfloat16 [16384, 1024], P(('pod', 'data', 'expert')), parts along dimension 0
- output 2: bfloat16 [16384, 1024], P(('pod', 'data', 'expert')), parts along dimension 0
- output 3: float32 [64, 1024, 512], P(('pod', 'expert')), parts along dimension 0
- output 4: float32 [64, 1024, 512], P(('pod', 'expert')), parts along dimension 0
- output 5: float32 [64, 512, 1024], P(('pod', 'expert')), parts along dimension 0
There are 2 independent parts. A program takes and returns all parts, laid end to end along the dimension named above; an argument that names none is the same for every part.
All inputs are finite; a program needn't handle non-finite values.
Results may differ from a plain program's by a relative error of at most 0.0106931.
Values are sent between devices in bfloat16 or wider.
A program may use at most 1 GiB of HBM per device.

v0:
```python
import jax
import jax.numpy as jnp
from jax import lax
from jax.sharding import PartitionSpec as P

N_HOT = 2


def value_a10(tok_dev, top_k, n_exp):
    cap_hot = 3 * tok_dev // 8
    cap_cold = max(8, ((tok_dev * top_k - N_HOT * cap_hot) // (n_exp - N_HOT) + 7) // 8 * 8)
    return cap_cold, cap_hot


def route_rows(routes_dev, n_exp, cap_cold, cap_hot):
    flat_exp = routes_dev.reshape(-1)
    n_slots = flat_exp.shape[0]
    order = jnp.argsort(flat_exp, stable=True)
    counts = jax.ops.segment_sum(jnp.ones((n_slots,), jnp.int32), flat_exp, num_segments=n_exp)
    starts = jnp.cumsum(counts) - counts
    rank_sorted = jnp.arange(n_slots, dtype=jnp.int32) - starts[flat_exp[order]]
    slot_rank = jnp.zeros((n_slots,), jnp.int32).at[order].set(rank_sorted)
    hot_index = jnp.where(flat_exp == 0, 0, jnp.where(flat_exp == n_exp // 2, 1, -1))
    cold_row = jnp.where((hot_index < 0) & (slot_rank < cap_cold), flat_exp * cap_cold + slot_rank, n_exp * cap_cold)
    hot_row = jnp.where(hot_index >= 0, hot_index * cap_hot + slot_rank, N_HOT * cap_hot)
    return cold_row, hot_row


def gather_rows(slot_rows, x_local, dy_local, gate_flat, n_rows):
    n_slots = slot_rows.shape[0]
    tok_n = x_local.shape[0]
    top_k = n_slots // tok_n
    src_tok = jnp.full((n_rows,), tok_n, jnp.int32).at[slot_rows].set(
        jnp.arange(n_slots, dtype=jnp.int32) // top_k, mode='drop')
    src_gate = jnp.zeros((n_rows,), jnp.float32).at[slot_rows].set(gate_flat, mode='drop')
    x_rows = jnp.take(x_local, src_tok, axis=0, mode='fill', fill_value=0)
    dy_rows = jnp.take(dy_local, src_tok, axis=0, mode='fill', fill_value=0)
    do_rows = (dy_rows.astype(jnp.float32) * src_gate[:, None]).astype(jnp.bfloat16)
    return x_rows, do_rows


def expert_fwd(x_rows, w_a, w_b, w_c):
    pre_a = jnp.einsum('esd,edf->esf', x_rows, w_a, preferred_element_type=jnp.float32).astype(jnp.bfloat16)
    pre_b = jnp.einsum('esd,edf->esf', x_rows, w_b, preferred_element_type=jnp.float32).astype(jnp.bfloat16)
    act_a = pre_a.astype(jnp.float32)
    hidden = (act_a * jax.nn.sigmoid(act_a) * pre_b.astype(jnp.float32)).astype(jnp.bfloat16)
    outs = jnp.einsum('esf,efd->esd', hidden, w_c, preferred_element_type=jnp.float32).astype(jnp.bfloat16)
    return outs, pre_a, pre_b, hidden


def expert_bwd(x_rows, do_rows, pre_a, pre_b, hidden, w_a, w_b, w_c):
    d_hidden = jnp.einsum('esd,efd->esf', do_rows, w_c, preferred_element_type=jnp.float32)
    act_a = pre_a.astype(jnp.float32)
    act_b = pre_b.astype(jnp.float32)
    sigma_a = jax.nn.sigmoid(act_a)
    d_pre_b = (d_hidden * act_a * sigma_a).astype(jnp.bfloat16)
    d_pre_a = (d_hidden * act_b * sigma_a * (1.0 + act_a * (1.0 - sigma_a))).astype(jnp.bfloat16)
    d_rows = (jnp.einsum('esf,edf->esd', d_pre_a, w_a, preferred_element_type=jnp.float32)
              + jnp.einsum('esf,edf->esd', d_pre_b, w_b, preferred_element_type=jnp.float32)).astype(jnp.bfloat16)
    grad_a = jnp.einsum('esd,esf->edf', x_rows, d_pre_a, preferred_element_type=jnp.float32)
    grad_b = jnp.einsum('esd,esf->edf', x_rows, d_pre_b, preferred_element_type=jnp.float32)
    grad_c = jnp.einsum('esf,esd->efd', hidden, do_rows, preferred_element_type=jnp.float32)
    return d_rows, grad_a, grad_b, grad_c


def combine(cold_rows, hot_rows, cold_vals, hot_vals, weights, tok_n):
    slot_vals = (jnp.take(cold_vals, cold_rows, axis=0, mode='fill', fill_value=0)
                 + jnp.take(hot_vals, hot_rows, axis=0, mode='fill', fill_value=0))
    slot_vals = slot_vals.reshape(tok_n, -1, cold_vals.shape[1]).astype(jnp.float32)
    if weights is not None:
        slot_vals = slot_vals * weights[:, :, None]
    return jnp.sum(slot_vals, axis=1).astype(jnp.bfloat16)


def solution(mesh):
    n_dev = mesh.shape['expert']
    row_spec = P(('pod', 'data', 'expert'), None)
    w_spec = P('expert', None, None)
    grad_spec = P(('pod', 'expert'), None, None)

    def body(tokens, routes, gates, grad_y, w_in1, w_in3, w_out):
        tok_n, d_model = tokens.shape
        top_k = routes.shape[1]
        exp_local = w_in1.shape[0]
        n_exp = exp_local * n_dev
        my_index = lax.axis_index('expert')
        cap_cold, cap_hot = value_a10(tok_n, top_k, n_exp)
        cold_rows, hot_rows = route_rows(routes, n_exp, cap_cold, cap_hot)
        gate_flat = gates.reshape(-1)
        cold_x, cold_do = gather_rows(cold_rows, tokens, grad_y, gate_flat, n_exp * cap_cold)
        hot_x, hot_do = gather_rows(hot_rows, tokens, grad_y, gate_flat, N_HOT * cap_hot)
        hot_x = hot_x.reshape(N_HOT, cap_hot, d_model)
        hot_do = hot_do.reshape(N_HOT, cap_hot, d_model)
        hot_local = [0, (n_exp // 2) % exp_local]
        hot_owner = [0, (n_exp // 2) // exp_local]

        def owned_copy(w_local):
            return jnp.stack([jnp.where(my_index == owner_idx, w_local[local_idx], 0)
                              for local_idx, owner_idx in zip(hot_local, hot_owner)])

        hot_w1, hot_w3, hot_w2 = lax.psum((owned_copy(w_in1), owned_copy(w_in3), owned_copy(w_out)), 'expert')

        recv_x = lax.all_to_all(cold_x.reshape(n_exp, cap_cold, d_model), 'expert', 0, 1, tiled=True)
        cold_out, cold_pre_a, cold_pre_b, cold_hidden = expert_fwd(recv_x, w_in1, w_in3, w_out)
        back_out = lax.all_to_all(cold_out, 'expert', 1, 0, tiled=True)
        hot_out, hot_pre_a, hot_pre_b, hot_hidden = expert_fwd(hot_x, hot_w1, hot_w3, hot_w2)
        y_out = combine(cold_rows, hot_rows, back_out.reshape(-1, d_model), hot_out.reshape(-1, d_model), gates, tok_n)

        recv_do = lax.all_to_all(cold_do.reshape(n_exp, cap_cold, d_model), 'expert', 0, 1, tiled=True)
        cold_dx, grad_w1, grad_w3, grad_w2 = expert_bwd(recv_x, recv_do, cold_pre_a, cold_pre_b, cold_hidden, w_in1, w_in3, w_out)
        back_dx = lax.all_to_all(cold_dx, 'expert', 1, 0, tiled=True)
        hot_dx, part_w1, part_w3, part_w2 = expert_bwd(hot_x, hot_do, hot_pre_a, hot_pre_b, hot_hidden, hot_w1, hot_w3, hot_w2)
        grad_x = combine(cold_rows, hot_rows, back_dx.reshape(-1, d_model), hot_dx.reshape(-1, d_model), None, tok_n)
        part_w1, part_w3, part_w2 = lax.psum((part_w1, part_w3, part_w2), 'expert')

        def add_owned(grad_local, hot_sum):
            for slot_h in range(N_HOT):
                grad_local = grad_local.at[hot_local[slot_h]].add(
                    jnp.where(my_index == hot_owner[slot_h], hot_sum[slot_h], 0.0))
            return grad_local

        grad_w1 = add_owned(grad_w1, part_w1)
        grad_w3 = add_owned(grad_w3, part_w3)
        grad_w2 = add_owned(grad_w2, part_w2)
        grad_w1, grad_w3, grad_w2 = lax.psum((grad_w1, grad_w3, grad_w2), 'data')
        return y_out, grad_x, grad_w1, grad_w3, grad_w2

    return jax.shard_map(body, mesh=mesh,
                         in_specs=(row_spec, row_spec, row_spec, row_spec, w_spec, w_spec, w_spec),
                         out_specs=(row_spec, row_spec, grad_spec, grad_spec, grad_spec),
                         check_vma=False)
```

profile of v0, /device:TPU:0, one launch (start us, length us, event | category | flops | bytes accessed | tf_op | source)
XLA Modules:
  0.0 2353.6 jit_solution(7114717296740225598)
XLA Ops:
  8.3 28.8 %scatter_custom_fusion = s32[32]{0:T(128)S(1)} fusion(s32[4096]{0:T(1024)S(1)} %reshape.276, s32[4096]{0:T(1024)S(1)} %broadcast_in_dim.109, s32[]{:T(128)} %constant.212.clone.1), kind=kCustom, calls=%fused_computation.160 | custom fusion | flops 4096 | bytes 132 | tf_op jit(solution)/shard_map/scatter-add | solution.py:19
  44.6 23.0 gather_fusion
  73.2 15.8 select_subtract_fusion
  89.0 15.5 scatter_custom_fusion.1
  105.1 15.5 scatter_custom_fusion.2
  120.7 18.1 gather_fusion.1
  160.8 15.5 scatter_custom_fusion.3
  176.3 15.7 scatter_custom_fusion.5
  192.0 15.5 scatter_custom_fusion.4
  212.3 18.1 gather_fusion.5
  238.4 70.7 %all-to-all-done = bf16[32,128,1024]{2,1,0:T(8,128)(2,1)} async-done(((bf16[32,128,1024]{2,1,0:T(8,128)(2,1)}), bf16[32,128,1024]{2,1,0:T(8,128)(2,1)}, u32[]{:S(2)}, u32[]{:S(2)}) %all-to-all-start) | async-done | bytes 8388640 | tf_op jit(solution)/shard_map/all_to_all | solution.py:103
  315.3 60.1 %all-reduce.11.cloned.1.call-done = (bf16[2,512,1024]{2,1,0:T(8,128)(2,1)}, bf16[2,1024,512]{2,1,0:T(8,128)(2,1)}, bf16[2,1024,512]{2,1,0:T(8,128)(2,1)}) async-done(((bf16[2,512,1024]{2,1,0:T(8,128)(2,1)}, bf16[2,1024,512]{2,1,0:T(8,128)(2,1)}, bf16[2,1024,512]{2,1,0:T(8,128)(2,1)}), (bf16[2,512,1024]{2,1,0:T(8,128)(2,1)}, bf16[2,1024,512]{2,1,0:T(8,128)(2,1)}, ...) | async-done | bytes 6291472 | tf_op jit(solution)/shard_map/psum | solution.py:101
  400.3 12.4 convolution_convert_fusion.2
  422.3 50.4 %all-to-all-done.2 = bf16[32,128,1024]{2,1,0:T(8,128)(2,1)} async-done(((bf16[32,128,1024]{2,1,0:T(8,128)(2,1)}), bf16[32,128,1024]{2,1,0:T(8,128)(2,1)}, u32[]{:S(2)}, u32[]{:S(2)}) %all-to-all-start.2) | async-done | bytes 8388640 | tf_op jit(solution)/shard_map/all_to_all | solution.py:109
  480.9 15.7 fusion.4
  496.6 15.8 fusion.62
  512.4 12.1 copy.52
  524.6 15.3 fusion.70
  551.4 16.4 fusion.59
  567.8 12.0 copy.56
  579.8 70.7 %all-reduce.7.cloned.1.call-done = (f32[2,1024,512]{2,1,0:T(8,128)}, f32[2,1024,512]{2,1,0:T(8,128)}, f32[2,512,1024]{2,1,0:T(8,128)}) async-done(((f32[2,1024,512]{2,1,0:T(8,128)}, f32[2,1024,512]{2,1,0:T(8,128)}, f32[2,512,1024]{2,1,0:T(8,128)}), (f32[2,1024,512]{2,1,0:T(8,128)}, f32[2,1024,512]{2,1,0:T(8,128)}, f32[2,512,1024]{2,1,0:T(8,128)})) %all-reduce.7.cloned.1.call-update) | async-done | bytes 12582928 | tf_op jit(solution)/shard_map/psum | solution.py:114
  671.3 14.2 convolution_convert_fusion
  703.1 15.4 fusion.67
  718.4 19.4 add_convert_fusion
  749.3 46.6 %all-to-all-done.1 = bf16[8,512,1024]{2,0,1:T(8,128)(2,1)} async-done(((bf16[8,512,1024]{2,0,1:T(8,128)(2,1)}), bf16[8,512,1024]{2,0,1:T(8,128)(2,1)}, u32[]{:S(2)}, u32[]{:S(2)}) %all-to-all-start.1) | async-done | bytes 8388640 | tf_op jit(solution)/shard_map/all_to_all | solution.py:105
  804.0 18.1 gather_fusion.4
  827.1 18.2 gather_fusion.8
  856.8 37.7 %all-to-all-done.3 = bf16[8,512,1024]{2,0,1:T(8,128)(2,1)} async-done(((bf16[8,512,1024]{2,0,1:T(8,128)(2,1)}), bf16[8,512,1024]{2,0,1:T(8,128)(2,1)}, u32[]{:S(2)}, u32[]{:S(2)}) %all-to-all-start.3) | async-done | bytes 8388640 | tf_op jit(solution)/shard_map/all_to_all | solution.py:111
  905.9 25.5 %gather_fusion.2 = bf16[4096,1024]{1,0:T(8,128)(2,1)} fusion(bf16[4096,1024]{1,0:T(8,128)(2,1)} %bitcast.97, s32[4096]{0:T(1024)S(1)} %get-tuple-element.172), kind=kCustom, calls=%fused_computation.1.clone | custom fusion | bytes 16793600 | tf_op jit(solution)/shard_map/jit(_take)/gather | solution.py:67
  931.5 25.2 %gather_fusion.6 = bf16[4096,1024]{1,0:T(8,128)(2,1)} fusion(bf16[4096,1024]{1,0:T(8,128)(2,1)} %bitcast.98, s32[4096]{0:T(1024)S(1)} %get-tuple-element.172), kind=kCustom, calls=%fused_computation.5.clone | custom fusion | bytes 16793600 | tf_op jit(solution)/shard_map/jit(_take)/gather | solution.py:67
  979.5 1333.7 %all-reduce.9.cloned.1.call-done = (f32[8,1024,512]{2,1,0:T(8,128)}, f32[8,1024,512]{2,1,0:T(8,128)}, f32[8,512,1024]{2,1,0:T(8,128)}) async-done(((f32[8,1024,512]{2,1,0:T(8,128)}, f32[8,1024,512]{2,1,0:T(8,128)}, f32[8,512,1024]{2,1,0:T(8,128)}), (f32[8,1024,512]{2,1,0:T(8,128)}, f32[8,1024,512]{2,1,0:T(8,128)}, f32[8,512,1024]{2,1,0:T(8,128)})) %all-reduce.9.cloned.1.call-update) | async-done | bytes 50331664 | tf_op jit(solution)/shard_map/psum | solution.py:125
  2313.1 13.5 copy.61
  (135 shorter events, 238.4 us)
Async XLA Ops:
  7.2 113.5 %copy-start = (bf16[512,1024]{1,0:T(8,128)(2,1)S(1)}, bf16[512,1024]{1,0:T(8,128)(2,1)}, u32[]{:S(2)}) copy-start(bf16[512,1024]{1,0:T(8,128)(2,1)} %param.27) | copy-start | bytes 3145732
  105.1 71.2 %copy-start.22 = (s32[4096]{0:T(1024)}, s32[4096]{0:T(1024)S(1)}, u32[]{:S(2)}) copy-start(s32[4096]{0:T(1024)S(1)} %get-tuple-element.130) | copy-start | bytes 49156
  105.1 86.9 %copy-start.20 = (s32[4096]{0:T(1024)}, s32[4096]{0:T(1024)S(1)}, u32[]{:S(2)}) copy-start(s32[4096]{0:T(1024)S(1)} %get-tuple-element.118) | copy-start | bytes 49156
  146.1 162.9 %all-to-all-start = ((bf16[32,128,1024]{2,1,0:T(8,128)(2,1)}), bf16[32,128,1024]{2,1,0:T(8,128)(2,1)}, u32[]{:S(2)}, u32[]{:S(2)}) async-start(bf16[32,128,1024]{2,1,0:T(8,128)(2,1)} %bitcast.103), calls=%async_computation | async-start | bytes 16777216 | tf_op jit(solution)/shard_map/all_to_all | solution.py:103
  151.8 223.6 %all-reduce.11.cloned.1.call-start = ((), (), s32[]{:S(2)}) async-start(), calls=%async_computation.6 | async-start | bytes 12582912 | tf_op jit(solution)/shard_map/psum | solution.py:101
  159.0 51.3 %copy-start.2 = (bf16[512,1024]{1,0:T(8,128)(2,1)S(1)}, bf16[512,1024]{1,0:T(8,128)(2,1)}, u32[]{:S(2)}) copy-start(bf16[512,1024]{1,0:T(8,128)(2,1)} %param.30) | copy-start | bytes 3145732
  160.6 46.9 %copy-start.14 = (f32[512,8]{1,0:T(8,128)}, f32[512,8]{1,0:T(8,128)S(1)}, u32[]{:S(2)}) copy-start(f32[512,8]{1,0:T(8,128)S(1)} %copy.35) | copy-start | bytes 49156
  309.0 163.7 %all-to-all-start.2 = ((bf16[32,128,1024]{2,1,0:T(8,128)(2,1)}), bf16[32,128,1024]{2,1,0:T(8,128)(2,1)}, u32[]{:S(2)}, u32[]{:S(2)}) async-start(bf16[32,128,1024]{2,1,0:T(8,128)(2,1)} %bitcast.104), calls=%async_computation.2 | async-start | bytes 16777216 | tf_op jit(solution)/shard_map/all_to_all | solution.py:109
  314.9 335.7 %all-reduce.7.cloned.1.call-start = ((), (), s32[]{:S(2)}) async-start(), calls=%async_computation.4 | async-start | bytes 25165824 | tf_op jit(solution)/shard_map/psum | solution.py:114
  377.8 11.5 copy-start.9
  380.3 9.0 copy-start.11
  392.1 1921.0 %all-reduce.9.cloned.1.call-start = ((), (), s32[]{:S(2)}) async-start(), calls=%async_computation.5 | async-start | bytes 100663296 | tf_op jit(solution)/shard_map/psum | solution.py:125
  400.3 12.4 copy-start.3
  650.5 8.1 copy-start.8
  654.8 7.2 copy-start.7
  697.4 98.5 %all-to-all-start.1 = ((bf16[8,512,1024]{2,0,1:T(8,128)(2,1)}), bf16[8,512,1024]{2,0,1:T(8,128)(2,1)}, u32[]{:S(2)}, u32[]{:S(2)}) async-start(bf16[8,512,1024]{2,0,1:T(8,128)(2,1)} %copy.33), calls=%async_computation.1 | async-start | bytes 16777216 | tf_op jit(solution)/shard_map/all_to_all | solution.py:105
  749.2 52.4 %copy-start.21 = (s32[4096]{0:T(1024)S(1)}, s32[4096]{0:T(1024)}, u32[]{:S(2)}) copy-start(s32[4096]{0:T(1024)} %copy-done.20) | copy-start | bytes 49156
  749.2 52.5 %copy-start.23 = (s32[4096]{0:T(1024)S(1)}, s32[4096]{0:T(1024)}, u32[]{:S(2)}) copy-start(s32[4096]{0:T(1024)} %copy-done.22) | copy-start | bytes 49156
  749.3 52.5 %copy-start.12 = (f32[2,192,512]{2,1,0:T(8,128)S(1)}, f32[2,192,512]{2,1,0:T(8,128)}, u32[]{:S(2)}) copy-start(f32[2,192,512]{2,1,0:T(8,128)} %copy-done.11) | copy-start | bytes 2359300
  749.3 52.5 %copy-start.17 = (bf16[2,192,512]{2,1,0:T(8,128)(2,1)S(1)}, bf16[2,192,512]{2,1,0:T(8,128)(2,1)}, u32[]{:S(2)}) copy-start(bf16[2,192,512]{2,1,0:T(8,128)(2,1)} %copy-done.16) | copy-start | bytes 1179652
  795.9 98.6 %all-to-all-start.3 = ((bf16[8,512,1024]{2,0,1:T(8,128)(2,1)}), bf16[8,512,1024]{2,0,1:T(8,128)(2,1)}, u32[]{:S(2)}, u32[]{:S(2)}) async-start(bf16[8,512,1024]{2,0,1:T(8,128)(2,1)} %copy.38), calls=%async_computation.3 | async-start | bytes 16777216 | tf_op jit(solution)/shard_map/all_to_all | solution.py:111
  804.0 18.2 copy-start.19
  804.0 20.6 copy-start.10
  931.4 25.3 %copy-start.24 = (pred[4096]{0:T(1024)(128)(4,1)S(1)}, pred[4096]{0:T(1024)(128)(4,1)}, u32[]{:S(2)}) copy-start(pred[4096]{0:T(1024)(128)(4,1)} %get-tuple-element.117) | copy-start | bytes 12292
  931.5 25.3 %copy-start.25 = (pred[4096]{0:T(1024)(128)(4,1)S(1)}, pred[4096]{0:T(1024)(128)(4,1)}, u32[]{:S(2)}) copy-start(pred[4096]{0:T(1024)(128)(4,1)} %get-tuple-element.129) | copy-start | bytes 12292
  956.7 11.1 copy-start.4
  956.7 11.1 copy-start.15
  2313.1 16.4 copy-start.5
  2313.1 24.9 %slice-start = ((s8[16777216]{0:T(1024)(128)(4,1)}), s8[4194304]{0:T(1024)(128)(4,1)S(1)}, s32[]{:S(2)}) async-start(s8[16777216]{0:T(1024)(128)(4,1)} %bitcast.105), calls=%async_computation.7 | async-start | bytes 8388608
  2313.1 24.9 %slice-start.1 = ((s8[16777216]{0:T(1024)(128)(4,1)}), s8[4194304]{0:T(1024)(128)(4,1)S(1)}, s32[]{:S(2)}) async-start(s8[16777216]{0:T(1024)(128)(4,1)} %bitcast.105), calls=%async_computation.8 | async-start | bytes 8388608
  2329.6 9.9 slice-start.2
  2329.6 11.1 slice-start.3
  (6 other events, 27.9 us)
Sparse Core Ops, SparseCore 0:
  160.6 214.7 all-reduce.10
  392.2 258.2 all-reduce.6
  671.5 1641.6 all-reduce.8
where the time goes:
time: 2360 us; the launch traced here: 2350 us
  waiting for transfers between devices  1670 us (71%)
  local copies, waits for them, and re-layouts  365 us (15%)
  matrix products  157 us (7%)
  other arithmetic  124 us (5%)
    psum x1, waiting for transfers between devices, body(): grad_w1, grad_w3, grad_w2 = lax.psum((grad_w1, grad_w3, grad_w2), 'data')  1330 us
    unnamed x70, local copies, waits for them, and re-layouts  71.2 us
    psum x1, waiting for transfers between devices, body(): part_w1, part_w3, part_w2 = lax.psum((part_w1, part_w3, part_w2), 'expert')  70.7 us
    all_to_all x1, waiting for transfers between devices, body(): lax.all_to_all(cold_x.reshape(n_exp, cap_cold, d_model), 'expert', 0, 1,...  70.7 us
    psum x1, waiting for transfers between devices, body(): lax.psum((owned_copy(w_in1), owned_copy(w_in3), owned_copy(w_out)), 'expe...  60.1 us
    gather x2, local copies, waits for them, and re-layouts, combine(): jnp.take(cold_vals, cold_rows, axis=0, mode='fill', fill_value=0)  50.8 us
    all_to_all x1, waiting for transfers between devices, body(): lax.all_to_all(cold_do.reshape(n_exp, cap_cold, d_model), 'expert', 0, 1,...  50.4 us
  transfers between devices with their start and end apart: 7, of which 7 were waited for; matrix products, arithmetic and copies ran while one was open for 19% of the time, Pallas kernels for 0%

commit v1 on v0

v1 whole, which is shorter than its diff:
```python
import functools

import jax
import jax.numpy as jnp
from jax import lax
from jax.experimental import pallas as pl
from jax.experimental.pallas import tpu as pltpu
from jax.sharding import PartitionSpec as P

N_HOT = 2
RG_ROWS = 16
F32, BF16 = jnp.float32, jnp.bfloat16


def caps(tok_dev, top_k, n_exp):
    cap_hot = 3 * tok_dev // 8
    cap_cold = max(8, ((tok_dev * top_k - N_HOT * cap_hot) // (n_exp - N_HOT) + 7) // 8 * 8)
    return cap_cold, cap_hot


def dot_nn(a, b):
    return lax.dot_general(a, b, (((1,), (0,)), ((), ())), preferred_element_type=F32)


def dot_nt(a, b):
    return lax.dot_general(a, b, (((1,), (1,)), ((), ())), preferred_element_type=F32)


def dot_tn(a, b):
    return lax.dot_general(a, b, (((0,), (0,)), ((), ())), preferred_element_type=F32)


def prefix(m):
    lane = lax.broadcasted_iota(jnp.int32, m.shape, 1)
    step = 1
    while step < m.shape[1]:
        m = m + jnp.where(lane >= step, pltpu.roll(m, step, 1), 0.0)
        step *= 2
    return m


def stage_kernel(cfg, *refs):
    n_src, n_own, first = cfg["n_src"], cfg["n_own"], cfg["first"]
    tok, d_model, n_loc, n_exp = cfg["tok"], cfg["d_model"], cfg["n_loc"], cfg["n_exp"]
    cap, extra = cfg["cap"], cfg["extra"]
    refs = list(refs)
    rank_ref = refs.pop(0)
    srcs = [refs.pop(0) for _ in range(n_src)]
    w1, w3, w2 = (refs.pop(0) for _ in range(3))
    acc = None if first else [refs.pop(0) for _ in range(3)]
    outs = [refs.pop(0) for _ in range(3)]
    part_y, part_x = (refs.pop(0), refs.pop(0)) if n_own else (None, None)
    rows_x, rows_d, meta, buf, sem = refs
    step = pl.program_id(0)
    lead = rank_ref[0, 0]

    def fetch(s, src):
        return pltpu.make_async_copy(src, buf.at[s % 2], sem.at[s % 2])

    @pl.when(step == 0)
    def _():
        fetch(0, srcs[0]).start()

    for s in range(n_src):
        @pl.when(step == s)
        def _(s=s):
            fetch(s, srcs[s]).wait()
            if s + 1 < n_src:
                fetch(s + 1, srcs[s + 1]).start()

    slot = step % 2

    @pl.when(step < n_src)
    def gather():
        rg = buf[slot, 2 * tok:2 * tok + RG_ROWS, :].astype(F32)
        routes = rg[0:8, :tok]
        gates = (rg[8:16, :tok] + rg[0:8, tok:]) + rg[8:16, tok:]
        member, weight = [], []
        for i in range(n_loc):
            match = routes == (lead * n_loc + i).astype(F32)
            member.append(jnp.sum(jnp.where(match, 1.0, 0.0), axis=0, keepdims=True))
            weight.append(jnp.sum(jnp.where(match, gates, 0.0), axis=0, keepdims=True))
        member = jnp.concatenate(member, axis=0)
        weight = jnp.concatenate(weight, axis=0)
        rank = jnp.where(member > 0.0, prefix(member) - 1.0, -1.0)
        meta[step, 0:8, :] = rank
        meta[step, 8:16, :] = weight
        x = buf[slot, 0:tok, :]
        dy = buf[slot, tok:2 * tok, :]

        def rows_of(i, base, size):
            iota = lax.broadcasted_iota(jnp.int32, (size, tok), 0).astype(F32) + base
            match = iota == meta[step, pl.ds(i, 1), :]
            gate = jnp.sum(jnp.where(match, meta[step, pl.ds(8 + i, 1), :], 0.0), axis=1, keepdims=True)
            return jnp.where(match, 1.0, 0.0).astype(BF16), gate

        def put(pick, gate, at, size):
            rows_x[step, pl.ds(at, size), :] = dot_nn(pick, x).astype(BF16)
            rows_d[step, pl.ds(at, size), :] = (dot_nn(pick, dy) * gate).astype(BF16)

        def pair(k, carry):
            p0, g0 = rows_of(2 * k, 0.0, cap)
            p1, g1 = rows_of(2 * k + 1, 0.0, cap)
            put(jnp.concatenate([p0, p1], axis=0), jnp.concatenate([g0, g1], axis=0),
                pl.multiple_of(2 * cap * k, 2 * cap), 2 * cap)
            return carry

        lax.fori_loop(0, n_loc // 2, pair, 0)
        lead_exp = lead * n_loc
        hot = jnp.logical_or(lead_exp == 0, lead_exp == n_exp // 2)
        far = jnp.where(hot, float(cap), float(2 * tok))
        p, g = rows_of(0, far, extra)
        put(p, g, n_loc * cap, extra)

    def block(at, size, fresh):
        xe = rows_x[:, pl.ds(at, size), :].reshape(n_src * size, d_model)
        de = rows_d[:, pl.ds(at, size), :].reshape(n_src * size, d_model)
        a = dot_nn(xe, w1[0]).astype(BF16).astype(F32)
        b = dot_nn(xe, w3[0]).astype(BF16).astype(F32)
        dh = dot_nt(de, w2[0])
        sig = 0.5 * jnp.tanh(0.5 * a) + 0.5
        act = a * sig
        h = (act * b).astype(BF16)
        db = (dh * act).astype(BF16)
        da = (dh * b * sig * (1.0 + a * (1.0 - sig))).astype(BF16)
        for out, base, lhs, rhs in zip(outs, acc or outs, (xe, xe, h), (da, db, de)):
            if fresh and first:
                out[0] = dot_tn(lhs, rhs)
            else:
                src = base if fresh else out
                out[0] = src[0] + dot_tn(lhs, rhs)
        if n_own:
            m = n_own * size
            o = dot_nn(h[:m], w2[0]).astype(BF16)
            dx = (dot_nt(da[:m], w1[0]) + dot_nt(db[:m], w3[0])).astype(BF16)
            rows_x[0:n_own, pl.ds(at, size), :] = o.reshape(n_own, size, d_model)
            rows_d[0:n_own, pl.ds(at, size), :] = dx.reshape(n_own, size, d_model)

    exp = step - n_src

    @pl.when(jnp.logical_and(exp >= 0, exp < n_loc))
    def main():
        block(pl.multiple_of(exp * cap, cap), cap, True)

    @pl.when(exp == 0)
    def more():
        block(n_loc * cap, extra, False)

    if n_own:
        src = exp - n_loc

        @pl.when(src >= 0)
        def combine():
            def weights_of(i, base, size):
                iota = lax.broadcasted_iota(jnp.int32, (size, tok), 0).astype(F32) + base
                match = iota == meta[src, pl.ds(i, 1), :]
                gate = meta[src, pl.ds(8 + i, 1), :]
                hi = gate.astype(BF16).astype(F32)
                mid = (gate - hi).astype(BF16).astype(F32)
                low = gate - hi - mid
                return [jnp.where(match, v, 0.0).astype(BF16) for v in (1.0, hi, mid, low)]

            def sums(pieces, at, size):
                o = rows_x[src, pl.ds(at, size), :]
                dx = rows_d[src, pl.ds(at, size), :]
                one, hi, mid, low = pieces
                return dot_tn(hi, o) + dot_tn(mid, o) + dot_tn(low, o), dot_tn(one, dx)

            lead_exp = lead * n_loc
            hot = jnp.logical_or(lead_exp == 0, lead_exp == n_exp // 2)
            far = jnp.where(hot, float(cap), float(2 * tok))
            py, px = sums(weights_of(0, far, extra), n_loc * cap, extra)
            part_y[0] = py
            part_x[0] = px

            def pair(k, carry):
                both = [jnp.concatenate(z, axis=0) for z in zip(weights_of(2 * k, 0.0, cap), weights_of(2 * k + 1, 0.0, cap))]
                py, px = sums(both, pl.multiple_of(2 * cap * k, 2 * cap), 2 * cap)
                part_y[0] += py
                part_x[0] += px
                return carry

            lax.fori_loop(0, n_loc // 2, pair, 0)


def run_stage(name, lead, srcs, weights, acc, n_own, n_exp):
    w1, w3, w2 = weights
    n_loc, d_model, d_ff = w1.shape
    tok = (srcs[0].shape[0] - RG_ROWS) // 2
    n_src = len(srcs)
    cap, cap_hot = caps(tok, 8, n_exp)
    extra = cap_hot - cap
    first = acc is None
    cfg = dict(n_src=n_src, n_own=n_own, first=first, tok=tok, d_model=d_model, n_loc=n_loc, n_exp=n_exp, cap=cap, extra=extra)
    per_exp = lambda i: (jnp.clip(i - n_src, 0, n_loc - 1), 0, 0)
    per_src = lambda i: (jnp.clip(i - n_src - n_loc, 0, max(n_own, 1) - 1), 0, 0)
    spec_in = pl.BlockSpec((1, d_model, d_ff), per_exp)
    spec_out = pl.BlockSpec((1, d_ff, d_model), per_exp)
    spec_tok = pl.BlockSpec((1, tok, d_model), per_src)
    in_specs = [pl.BlockSpec(memory_space=pltpu.SMEM)] + [pl.BlockSpec(memory_space=pl.ANY)] * n_src + [spec_in, spec_in, spec_out]
    args = [lead, *srcs, w1, w3, w2]
    aliases = {}
    if not first:
        for k in range(3):
            aliases[len(args) + k] = k
        in_specs += [spec_in, spec_in, spec_out]
        args += list(acc)
    shapes = [jax.ShapeDtypeStruct((n_loc, d_model, d_ff), F32)] * 2 + [jax.ShapeDtypeStruct((n_loc, d_ff, d_model), F32)]
    out_specs = [spec_in, spec_in, spec_out]
    if n_own:
        shapes += [jax.ShapeDtypeStruct((n_own, tok, d_model), F32)] * 2
        out_specs += [spec_tok, spec_tok]
    per_src_rows = n_loc * cap + extra
    unit = 2 * d_model * d_ff * per_src_rows
    return pl.pallas_call(
        functools.partial(stage_kernel, cfg),
        grid=(n_src + n_loc + n_own,),
        in_specs=in_specs,
        out_specs=out_specs,
        out_shape=shapes,
        input_output_aliases=aliases,
        scratch_shapes=[
            pltpu.VMEM((n_src, per_src_rows, d_model), BF16),
            pltpu.VMEM((n_src, per_src_rows, d_model), BF16),
            pltpu.VMEM((n_src, 16, tok), F32),
            pltpu.VMEM((2, 2 * tok + RG_ROWS, d_model), BF16),
            pltpu.SemaphoreType.DMA((2,)),
        ],
        compiler_params=pltpu.CompilerParams(vmem_limit_bytes=67_000_000, dimension_semantics=("arbitrary",)),
        cost_estimate=pl.CostEstimate(flops=unit * (8 * n_src + 7 * n_own) // 8, bytes_accessed=100 << 20, transcendentals=0),
        name=name,
    )(*args)


def solution(mesh):
    n_data, n_er = mesh.shape["data"], mesh.shape["expert"]
    row_spec = P(("pod", "data", "expert"), None)
    w_spec = P("expert", None, None)
    grad_spec = P(("pod", "expert"), None, None)
    partner = [(r, r ^ 1) for r in range(n_er)]
    across = [(r, r ^ 2) for r in range(n_er)]
    around = [(q, (q + 1) % n_data) for q in range(n_data)]

    def body(tokens, routes, gates, grad_y, w_in1, w_in3, w_out):
        n_exp = w_in1.shape[0] * n_er
        lead = lax.axis_index("expert").astype(jnp.int32).reshape(1, 1)
        gate = gates.T
        hi = lax.reduce_precision(gate, 8, 7)
        mid = lax.reduce_precision(gate - hi, 8, 7)
        low = gate - hi - mid
        rg = jnp.concatenate([jnp.concatenate([routes.T.astype(F32), hi], 0), jnp.concatenate([mid, low], 0)], 1)
        pack = jnp.concatenate([tokens, grad_y, rg.astype(BF16)], 0)

        to_partner = lambda v: lax.ppermute(v, "expert", partner)
        to_across = lambda v: lax.ppermute(v, "expert", across)
        to_next = lambda v: lax.ppermute(v, "data", around)

        here, other, far, zed = pack, to_partner(pack), to_across(pack), to_next(pack)
        weights = (w_in1, w_in3, w_out)
        acc1, acc3, acc2, py0, px0 = run_stage("own_chip", lead, [here, other], weights, None, 2, n_exp)
        acc1, acc3, acc2, far, zed = lax.optimization_barrier((acc1, acc3, acc2, far, zed))
        far_other = to_partner(far)
        acc1, acc3, acc2, py1, px1 = run_stage("near_chip", lead, [far, far_other], weights, (acc1, acc3, acc2), 2, n_exp)
        got, got_far = to_partner(jnp.stack([py0[1], px0[1]])), to_partner(jnp.stack([py1[1], px1[1]]))
        for k in range(n_data - 1):
            yed, zed_other = to_across(zed), to_partner(zed)
            after = to_next(zed) if k + 2 < n_data else zed
            acc1, acc3, acc2, zed, zed_other, yed, after = lax.optimization_barrier((acc1, acc3, acc2, zed, zed_other, yed, after))
            if k == 1:
                got_far, acc1 = lax.optimization_barrier((got_far, acc1))
                back = to_across(jnp.stack([py1[0] + got_far[0], px1[0] + got_far[1]]))
            block = [zed, zed_other, yed, to_partner(yed)]
            acc1, acc3, acc2 = run_stage(f"hop{k}", lead, block, weights, (acc1, acc3, acc2), 0, n_exp)
            zed = after

        y_out = (py0[0] + got[0] + back[0]).astype(BF16)
        grad_x = (px0[0] + got[1] + back[1]).astype(BF16)
        return y_out, grad_x, acc1, acc3, acc2

    return jax.shard_map(body, mesh=mesh,
                         in_specs=(row_spec, row_spec, row_spec, row_spec, w_spec, w_spec, w_spec),
                         out_specs=(row_spec, row_spec, grad_spec, grad_spec, grad_spec),
                         check_vma=False)
```

time: 2360 us -> 404 us (0.17)
  waiting for transfers between devices: 1670 us -> 6.87 us
  local copies, waits for them, and re-layouts: 365 us -> 6.08 us
  Pallas kernels: 0 us -> 341 us
  matrix products: 157 us -> 0 us
  other arithmetic: 124 us -> 25.2 us
    psum x3 -> x0, waiting for transfers between devices: 1460 us -> none  [the longest x1 1330 us: body(): grad_w1, grad_w3, grad_w2 = lax.psum((grad_w1, grad_w3, grad_w2), 'data')]
    pallas_call x0 -> x5, Pallas kernels: none -> 341 us  [run_stage(): pl.pallas_call(functools.partial(stage_kernel, cfg), grid=(n_src + n_loc...]
    all_to_all x4 -> x0, waiting for transfers between devices: 205 us -> none  [the longest x1 70.7 us: body(): lax.all_to_all(cold_x.reshape(n_exp, cap_cold, d_model), 'expert', 0, 1,...]
    dot_general x18 -> x0, matrix products: 157 us -> none  [the longest x2 21.9 us: expert_bwd(): jnp.einsum('esf,edf->esd', d_pre_b, w_b, preferred_element_type=jnp.float32)]
    gather x11 -> x0, local copies, waits for them, and re-layouts: 153 us -> none  [the longest x2 50.8 us: combine(): jnp.take(cold_vals, cold_rows, axis=0, mode='fill', fill_value=0)]
    scatter x5 -> x0, local copies, waits for them, and re-layouts: 77.7 us -> none  [the longest x2 31.2 us: gather_rows(): jnp.zeros((n_rows,), jnp.float32).at[slot_rows].set(gate_flat, mode='drop')]
    unnamed x70 -> x10, local copies, waits for them, and re-layouts: 71.2 us -> 0.94 us
    scatter-add x6 -> x0, other arithmetic: 49.6 us -> none  [the longest x1 28.8 us: route_rows(): jax.ops.segment_sum(jnp.ones((n_slots,), jnp.int32), flat_exp, num_segmen...]
  transfers between devices with their start and end apart: 7 -> 18, of which waited for: 7 -> 2; matrix products, arithmetic and copies ran while one was open for 19% -> 5% of each run, Pallas kernels for 0% -> 86%
where the time goes in v1:
time: 404 us; the launch traced here: 397 us
  Pallas kernels  341 us (84%)
  other arithmetic  25.2 us (6%)
  starting transfers between devices  16.8 us (4%)
  waiting for transfers between devices  6.87 us (2%)
  local copies, waits for them, and re-layouts  6.08 us (2%)
    pallas_call x5, Pallas kernels, run_stage(): pl.pallas_call(functools.partial(stage_kernel, cfg), grid=(n_src + n_loc...  341 us
    ppermute x5, starting transfers between devices, body(): to_across = lambda v: lax.ppermute(v, 'expert', across)  9.09 us
  transfers between devices with their start and end apart: 18, of which 2 were waited for; matrix products, arithmetic and copies ran while one was open for 5% of the time, Pallas kernels for 86%

profile of v1, /device:TPU:0, one launch (start us, length us, event | category | flops | bytes accessed | tf_op | source)
XLA Modules:
  0.0 396.9 jit_solution(7932906366768935642)
XLA Ops:
  0.6 0.7 reduce-precision_convert_fusion.1
  1.4 0.7 fusion.5
  2.1 3.7 maximum_maximum_fusion.refs_1_
  5.8 0.5 collective-permute-start
  6.3 2.5 collective-permute-start.2
  8.8 1.6 collective-permute-start.3
  10.4 58.8 %own_chip.1 = (f32[8,1024,512]{2,1,0:T(8,128)}, f32[8,1024,512]{2,1,0:T(8,128)}, f32[8,512,1024]{2,1,0:T(8,128)}, f32[2,512,1024]{2,1,0:T(8,128)}, f32[2,512,1024]{2,1,0:T(8,128)}) custom-call(s32[1,1]{1,0:T(1,128)} %bitcast.refs_0_, bf16[1040,1024]{1,0:T(8,128)(2,1)} %maximum_maximum_fusion.refs_1_, bf16[1040,1024]{1,0:T(8,128)(2,1)} %collective-permute-done.refs_2_, ...), custom_call_target="tpu_custom_call" | custom-call | flops 4278190080 | bytes 104857600 | tf_op jit(solution)/shard_map/own_chip/pallas_call | solution.py:215
  69.4 0.5 collective-permute-start.6
  69.8 2.6 collective-permute-start.7
  72.4 1.7 collective-permute-start.8
  74.1 72.5 %near_chip.1 = (f32[8,1024,512]{2,1,0:T(8,128)}, f32[8,1024,512]{2,1,0:T(8,128)}, f32[8,512,1024]{2,1,0:T(8,128)}, f32[2,512,1024]{2,1,0:T(8,128)}, f32[2,512,1024]{2,1,0:T(8,128)}) custom-call(s32[1,1]{1,0:T(1,128)} %bitcast.refs_0_, bf16[1040,1024]{1,0:T(8,128)(2,1)} %collective-permute-done.2.refs_1_, ...), custom_call_target="tpu_custom_call", output_to_operand_aliasing={{0}: (6, {}), {1}: (7, {}), {2}: (8, {})} | custom-call | flops 4278190080 | bytes 104857600 | tf_op jit(solution)/shard_map/near_chip/pallas_call | solution.py:215
  146.7 1.9 slice.48
  148.6 0.9 copy-done.2
  149.5 0.2 slice.47
  149.7 2.4 pad_maximum_fusion.1
  152.2 0.6 collective-permute-start.9
  152.8 2.0 collective-permute-start.11
  154.8 1.8 collective-permute-start.12
  156.6 1.5 slice.44
  158.1 1.5 slice.43
  159.6 2.7 collective-permute-done.9.refs_4_
  162.3 69.7 %hop0.1 = (f32[8,1024,512]{2,1,0:T(8,128)}, f32[8,1024,512]{2,1,0:T(8,128)}, f32[8,512,1024]{2,1,0:T(8,128)}) custom-call(s32[1,1]{1,0:T(1,128)} %bitcast.refs_0_, bf16[1040,1024]{1,0:T(8,128)(2,1)} %collective-permute-done.3.refs_1_, bf16[1040,1024]{1,0:T(8,128)(2,1)} %collective-permute-done.6.refs_2_, ...), custom_call_target="tpu_custom_call", output_to_operand_aliasing={{0}: (8, {}), {1}: (9, {}), {2}: (10, {})} | custom-call | flops 4563402752 | bytes 104857600 | tf_op jit(solution)/shard_map/hop0/pallas_call | solution.py:215
  232.1 0.3 collective-permute-start.14
  232.3 5.0 %pad_maximum_fusion = f32[2,512,1024]{2,1,0:T(8,128)} fusion(f32[1,512,1024]{2,1,0:T(8,128)} %slice.44, f32[1,512,1024]{2,1,0:T(8,128)} %slice.43), kind=kLoop, calls=%fused_computation | loop fusion | flops 1048576 | bytes 8388608 | tf_op jit(solution)/shard_map/stack | solution.py:264
  237.3 0.3 collective-permute-start.1
  237.8 1.9 collective-permute-start.16
  239.7 3.2 slice_add_fusion.5
  242.9 2.3 pad_maximum_fusion.2
  245.3 70.0 %hop1.1 = (f32[8,1024,512]{2,1,0:T(8,128)}, f32[8,1024,512]{2,1,0:T(8,128)}, f32[8,512,1024]{2,1,0:T(8,128)}) custom-call(s32[1,1]{1,0:T(1,128)} %bitcast.refs_0_, bf16[1040,1024]{1,0:T(8,128)(2,1)} %collective-permute-done.8.refs_1_, ...), custom_call_target="tpu_custom_call", output_to_operand_aliasing={{0}: (8, {}), {1}: (9, {}), {2}: (10, {})} | custom-call | flops 4563402752 | bytes 104857600 | tf_op jit(solution)/shard_map/hop1/pallas_call | solution.py:215
  315.4 4.1 %collective-permute-done.17.refs_4_ = bf16[1040,1024]{1,0:T(8,128)(2,1)} collective-permute-done((bf16[1040,1024]{1,0:T(8,128)(2,1)}, bf16[1040,1024]{1,0:T(8,128)(2,1)}, u32[]{:S(2)}, u32[]{:S(2)}) %collective-permute-start.17) | collective-permute-done | bytes 2129952 | tf_op jit(solution)/shard_map/ppermute | solution.py:254
  319.5 69.7 %hop2.1 = (f32[8,1024,512]{2,1,0:T(8,128)}, f32[8,1024,512]{2,1,0:T(8,128)}, f32[8,512,1024]{2,1,0:T(8,128)}) custom-call(s32[1,1]{1,0:T(1,128)} %bitcast.refs_0_, bf16[1040,1024]{1,0:T(8,128)(2,1)} %collective-permute-done.12.refs_1_, ...), custom_call_target="tpu_custom_call", output_to_operand_aliasing={{0}: (8, {}), {1}: (9, {}), {2}: (10, {})} | custom-call | flops 4563402752 | bytes 104857600 | tf_op jit(solution)/shard_map/hop2/pallas_call | solution.py:215
  389.2 7.2 %fusion.3 = (bf16[512,1024]{1,0:T(8,128)(2,1)}, bf16[512,1024]{1,0:T(8,128)(2,1)}) fusion(f32[2,512,1024]{2,1,0:T(8,128)} %collective-permute-done.13, f32[2,512,1024]{2,1,0:T(8,128)} %collective-permute-done.1, f32[2,512,1024]{2,1,0:T(8,128)} %get-tuple-element.52, f32[2,512,1024]{2,1,0:T(8,128)} %get-tuple-element.51), kind=kLoop, calls=%fused_computation.13 | loop fusion | flops 3145728 | bytes 14680064 | tf_op jit(solution)/shard_map/convert_element_type | solution.py:277
  (31 shorter events, 0.6 us)
Async XLA Ops:
  5.8 4.6 %collective-permute-start = (bf16[1040,1024]{1,0:T(8,128)(2,1)}, bf16[1040,1024]{1,0:T(8,128)(2,1)}, u32[]{:S(2)}, u32[]{:S(2)}) collective-permute-start(bf16[1040,1024]{1,0:T(8,128)(2,1)} %maximum_maximum_fusion.refs_1_), channel_id=1, source_target_pairs={{0,1},{1,0},{2,3},{3,2},{4,5},{5,4},{6,7},{7,6},{8,9},{9,8},{10,11... | collective-permute-start | bytes 6389768 | tf_op jit(solution)/shard_map/ppermute | solution.py:254
  6.3 62.9 %collective-permute-start.2 = (bf16[1040,1024]{1,0:T(8,128)(2,1)}, bf16[1040,1024]{1,0:T(8,128)(2,1)}, u32[]{:S(2)}, u32[]{:S(2)}) collective-permute-start(bf16[1040,1024]{1,0:T(8,128)(2,1)} %maximum_maximum_fusion.refs_1_), channel_id=1, source_target_pairs={{0,2},{1,3},{2,0},{3,1},{4,6},{5,7},{6,4},{7,5},{8,10},{9,11},{10,... | collective-permute-start | bytes 6389768 | tf_op jit(solution)/shard_map/ppermute | solution.py:255
  8.8 60.4 %collective-permute-start.3 = (bf16[1040,1024]{1,0:T(8,128)(2,1)}, bf16[1040,1024]{1,0:T(8,128)(2,1)}, u32[]{:S(2)}, u32[]{:S(2)}) collective-permute-start(bf16[1040,1024]{1,0:T(8,128)(2,1)} %maximum_maximum_fusion.refs_1_), channel_id=1, source_target_pairs={{0,4},{4,8},{8,12},{12,0},{1,5},{5,9},{9,13},{13,1},{2,6},{6,10},{... | collective-permute-start | bytes 6389768 | tf_op jit(solution)/shard_map/ppermute | solution.py:256
  69.2 4.9 %collective-permute-start.4 = (bf16[1040,1024]{1,0:T(8,128)(2,1)}, bf16[1040,1024]{1,0:T(8,128)(2,1)}, u32[]{:S(2)}, u32[]{:S(2)}) collective-permute-start(bf16[1040,1024]{1,0:T(8,128)(2,1)} %collective-permute-done.2.refs_1_), channel_id=1, source_target_pairs={{0,1},{1,0},{2,3},{3,2},{4,5},{5,4},{6,7},{7,6},{8,9},{9,8},{10,11... | collective-permute-start | bytes 6389768 | tf_op jit(solution)/shard_map/ppermute | solution.py:254
  69.4 82.8 %collective-permute-start.6 = (bf16[1040,1024]{1,0:T(8,128)(2,1)}, bf16[1040,1024]{1,0:T(8,128)(2,1)}, u32[]{:S(2)}, u32[]{:S(2)}) collective-permute-start(bf16[1040,1024]{1,0:T(8,128)(2,1)} %collective-permute-done.3.refs_1_), channel_id=1, source_target_pairs={{0,1},{1,0},{2,3},{3,2},{4,5},{5,4},{6,7},{7,6},{8,9},{9,8},{10,11... | collective-permute-start | bytes 6389768 | tf_op jit(solution)/shard_map/ppermute | solution.py:254
  69.8 82.4 %collective-permute-start.7 = (bf16[1040,1024]{1,0:T(8,128)(2,1)}, bf16[1040,1024]{1,0:T(8,128)(2,1)}, u32[]{:S(2)}, u32[]{:S(2)}) collective-permute-start(bf16[1040,1024]{1,0:T(8,128)(2,1)} %collective-permute-done.3.refs_1_), channel_id=1, source_target_pairs={{0,2},{1,3},{2,0},{3,1},{4,6},{5,7},{6,4},{7,5},{8,10},{9,11},{10,... | collective-permute-start | bytes 6389768 | tf_op jit(solution)/shard_map/ppermute | solution.py:255
  72.4 79.8 %collective-permute-start.8 = (bf16[1040,1024]{1,0:T(8,128)(2,1)}, bf16[1040,1024]{1,0:T(8,128)(2,1)}, u32[]{:S(2)}, u32[]{:S(2)}) collective-permute-start(bf16[1040,1024]{1,0:T(8,128)(2,1)} %collective-permute-done.3.refs_1_), channel_id=1, source_target_pairs={{0,4},{4,8},{8,12},{12,0},{1,5},{5,9},{9,13},{13,1},{2,6},{6,10},{... | collective-permute-start | bytes 6389768 | tf_op jit(solution)/shard_map/ppermute | solution.py:256
  146.7 2.8 copy-start.2
  149.7 6.9 %copy-start.1 = (f32[2,512,1024]{2,1,0:T(8,128)S(1)}, f32[2,512,1024]{2,1,0:T(8,128)}, u32[]{:S(2)}) copy-start(f32[2,512,1024]{2,1,0:T(8,128)} %get-tuple-element.52) | copy-start | bytes 12582916
  152.2 6.0 %copy-start = (f32[2,512,1024]{2,1,0:T(8,128)S(1)}, f32[2,512,1024]{2,1,0:T(8,128)}, u32[]{:S(2)}) copy-start(f32[2,512,1024]{2,1,0:T(8,128)} %get-tuple-element.51) | copy-start | bytes 12582916
  152.2 87.5 %collective-permute-start.5 = (f32[2,512,1024]{2,1,0:T(8,128)}, f32[2,512,1024]{2,1,0:T(8,128)}, u32[]{:S(2)}, u32[]{:S(2)}) collective-permute-start(f32[2,512,1024]{2,1,0:T(8,128)} %pad_maximum_fusion.1), channel_id=1, source_target_pairs={{0,1},{1,0},{2,3},{3,2},{4,5},{5,4},{6,7},{7,6},{8,9},{9,8},{10,11... | collective-permute-start | bytes 12582920 | tf_op jit(solution)/shard_map/ppermute | solution.py:254
  152.2 10.1 %collective-permute-start.9 = (bf16[1040,1024]{1,0:T(8,128)(2,1)}, bf16[1040,1024]{1,0:T(8,128)(2,1)}, u32[]{:S(2)}, u32[]{:S(2)}) collective-permute-start(bf16[1040,1024]{1,0:T(8,128)(2,1)} %collective-permute-done.7.refs_3_), channel_id=1, source_target_pairs={{0,1},{1,0},{2,3},{3,2},{4,5},{5,4},{6,7},{7,6},{8,9},{9,8},{10,11... | collective-permute-start | bytes 6389768 | tf_op jit(solution)/shard_map/ppermute | solution.py:254
  152.8 79.3 %collective-permute-start.10 = (bf16[1040,1024]{1,0:T(8,128)(2,1)}, bf16[1040,1024]{1,0:T(8,128)(2,1)}, u32[]{:S(2)}, u32[]{:S(2)}) collective-permute-start(bf16[1040,1024]{1,0:T(8,128)(2,1)} %collective-permute-done.8.refs_1_), channel_id=1, source_target_pairs={{0,1},{1,0},{2,3},{3,2},{4,5},{5,4},{6,7},{7,6},{8,9},{9,8},{10,11... | collective-permute-start | bytes 6389768 | tf_op jit(solution)/shard_map/ppermute | solution.py:254
  152.8 79.2 %collective-permute-start.11 = (bf16[1040,1024]{1,0:T(8,128)(2,1)}, bf16[1040,1024]{1,0:T(8,128)(2,1)}, u32[]{:S(2)}, u32[]{:S(2)}) collective-permute-start(bf16[1040,1024]{1,0:T(8,128)(2,1)} %collective-permute-done.8.refs_1_), channel_id=1, source_target_pairs={{0,2},{1,3},{2,0},{3,1},{4,6},{5,7},{6,4},{7,5},{8,10},{9,11},{10,... | collective-permute-start | bytes 6389768 | tf_op jit(solution)/shard_map/ppermute | solution.py:255
  154.8 77.2 %collective-permute-start.12 = (bf16[1040,1024]{1,0:T(8,128)(2,1)}, bf16[1040,1024]{1,0:T(8,128)(2,1)}, u32[]{:S(2)}, u32[]{:S(2)}) collective-permute-start(bf16[1040,1024]{1,0:T(8,128)(2,1)} %collective-permute-done.8.refs_1_), channel_id=1, source_target_pairs={{0,4},{4,8},{8,12},{12,0},{1,5},{5,9},{9,13},{13,1},{2,6},{6,10},{... | collective-permute-start | bytes 6389768 | tf_op jit(solution)/shard_map/ppermute | solution.py:256
  232.1 7.7 %copy-start.3 = (f32[2,512,1024]{2,1,0:T(8,128)S(1)}, f32[2,512,1024]{2,1,0:T(8,128)}, u32[]{:S(2)}) copy-start(f32[2,512,1024]{2,1,0:T(8,128)} %get-tuple-element.60) | copy-start | bytes 12582916
  232.1 7.6 %copy-start.4 = (f32[2,512,1024]{2,1,0:T(8,128)S(1)}, f32[2,512,1024]{2,1,0:T(8,128)}, u32[]{:S(2)}) copy-start(f32[2,512,1024]{2,1,0:T(8,128)} %get-tuple-element.61) | copy-start | bytes 12582916
  232.1 13.2 %collective-permute-start.14 = (bf16[1040,1024]{1,0:T(8,128)(2,1)}, bf16[1040,1024]{1,0:T(8,128)(2,1)}, u32[]{:S(2)}, u32[]{:S(2)}) collective-permute-start(bf16[1040,1024]{1,0:T(8,128)(2,1)} %collective-permute-done.11.refs_3_), channel_id=1, source_target_pairs={{0,1},{1,0},{2,3},{3,2},{4,5},{5,4},{6,7},{7,6},{8,9},{9,8},{10,11... | collective-permute-start | bytes 6389768 | tf_op jit(solution)/shard_map/ppermute | solution.py:254
  237.3 151.9 %collective-permute-start.1 = (f32[2,512,1024]{2,1,0:T(8,128)}, f32[2,512,1024]{2,1,0:T(8,128)}, u32[]{:S(2)}, u32[]{:S(2)}) collective-permute-start(f32[2,512,1024]{2,1,0:T(8,128)} %pad_maximum_fusion), channel_id=1, source_target_pairs={{0,1},{1,0},{2,3},{3,2},{4,5},{5,4},{6,7},{7,6},{8,9},{9,8},{10,11... | collective-permute-start | bytes 12582920 | tf_op jit(solution)/shard_map/ppermute | solution.py:254
  237.6 77.6 %collective-permute-start.15 = (bf16[1040,1024]{1,0:T(8,128)(2,1)}, bf16[1040,1024]{1,0:T(8,128)(2,1)}, u32[]{:S(2)}, u32[]{:S(2)}) collective-permute-start(bf16[1040,1024]{1,0:T(8,128)(2,1)} %collective-permute-done.12.refs_1_), channel_id=1, source_target_pairs={{0,1},{1,0},{2,3},{3,2},{4,5},{5,4},{6,7},{7,6},{8,9},{9,8},{10,11... | collective-permute-start | bytes 6389768 | tf_op jit(solution)/shard_map/ppermute | solution.py:254
  237.8 77.5 %collective-permute-start.16 = (bf16[1040,1024]{1,0:T(8,128)(2,1)}, bf16[1040,1024]{1,0:T(8,128)(2,1)}, u32[]{:S(2)}, u32[]{:S(2)}) collective-permute-start(bf16[1040,1024]{1,0:T(8,128)(2,1)} %collective-permute-done.12.refs_1_), channel_id=1, source_target_pairs={{0,2},{1,3},{2,0},{3,1},{4,6},{5,7},{6,4},{7,5},{8,10},{9,11},{10,... | collective-permute-start | bytes 6389768 | tf_op jit(solution)/shard_map/ppermute | solution.py:255
  245.2 144.0 %collective-permute-start.13 = (f32[2,512,1024]{2,1,0:T(8,128)}, f32[2,512,1024]{2,1,0:T(8,128)}, u32[]{:S(2)}, u32[]{:S(2)}) collective-permute-start(f32[2,512,1024]{2,1,0:T(8,128)} %pad_maximum_fusion.2), channel_id=1, source_target_pairs={{0,2},{1,3},{2,0},{3,1},{4,6},{5,7},{6,4},{7,5},{8,10},{9,11},{10,... | collective-permute-start | bytes 12582920 | tf_op jit(solution)/shard_map/ppermute | solution.py:255
  315.3 4.2 %collective-permute-start.17 = (bf16[1040,1024]{1,0:T(8,128)(2,1)}, bf16[1040,1024]{1,0:T(8,128)(2,1)}, u32[]{:S(2)}, u32[]{:S(2)}) collective-permute-start(bf16[1040,1024]{1,0:T(8,128)(2,1)} %collective-permute-done.16.refs_3_), channel_id=1, source_target_pairs={{0,1},{1,0},{2,3},{3,2},{4,5},{5,4},{6,7},{7,6},{8,9},{9,8},{10,11... | collective-permute-start | bytes 6389768 | tf_op jit(solution)/shard_map/ppermute | solution.py:254
